TPU v7x, 32 devices: a whole 2x2x4 slice. The times are simulated.
32 devices in a mesh: groups: 2 (over y), seq: 4 (over z), role: 2 (over x), mb: 2 (over core).
Axes of the slice: x: 2, y: 2, z: 4, core: 2. Of those that a mesh axis runs over, the one named last changes fastest.
Arguments:
- queries: bfloat16 [256, 128, 576], P(('groups', 'seq'), ('role', 'mb')), parts along dimension 0, may hold values from -200 to 200
- cache: bfloat16 [256, 256, 576], P(('groups', 'seq')), parts along dimension 0, may hold values from -24 to 24
- lengths: int32 [256], P(('groups', 'seq')), parts along dimension 0, may hold values from 2 to 256
- w_uv: bfloat16 [128, 512, 128], P(('role', 'mb'), None, 'seq'), may hold values from -0.25 to 0.25
- w_o: bfloat16 [128, 128, 3584], P(('role', 'mb'), 'seq'), may hold values from -0.1875 to 0.1875
- x_in: bfloat16 [256, 3584], P('groups', 'seq'), parts along dimension 0, may hold values from -16 to 16
- norm_gain: float32 [3584], P('seq'), may hold values from 0.1 to 1.9
- w_gate: bfloat16 [8, 3584, 2048], P(('seq', 'mb'), None, 'role'), may hold values from -0.09375 to 0.09375
- w_up: bfloat16 [8, 3584, 2048], P(('seq', 'mb'), None, 'role'), may hold values from -0.09375 to 0.09375
- w_down: bfloat16 [8, 2048, 3584], P(('seq', 'mb'), 'role'), may hold values from -0.125 to 0.125
- expert_ids: int32 [256, 2], P('groups'), parts along dimension 0, may hold values from 0 to 7, all different within a row; in each aligned block of 128 rows (0 to 127, 128 to 255, ...) at most 64 rows name the same one
- gate_weights: float32 [256, 2], P('groups'), parts along dimension 0, may hold values from 0.2 to 1
- expert_slot: int32 [8], replicated, may hold values from 0 to 7, each once
Outputs:
- layer_out: bfloat16 [256, 3584], P('groups', 'seq'), parts along dimension 0
There are 2 independent parts, one for each index of `groups`. A program takes and returns all parts, laid end to end along the dimension named above; an argument that names none is the same for every part. Nothing has to cross between parts.
Inputs may be any that keep to these rules, and one draw needn't show every extreme that they name: `expert_ids`: each row names 2 different experts; over the rows of one group no expert is named more than 64 times, a bound that some block reaches. A permutation: expert e uses the weights at index expert_slot[e].
All inputs are finite; a program needn't handle non-finite values.
Results may differ from a plain program's by a relative error of at most 0.012.
Values may be sent and summed in bfloat16 or wider, within the bound.
No kernel may reach another device: no remote copies, remote signals or barrier semaphores. Data moves between devices by JAX's collectives and lax.ppermute only.
A program may use at most 128 MiB of HBM per device.

v0:
```python
import jax
import jax.numpy as jnp
from jax import lax
from jax.sharding import PartitionSpec as P

D = 3584
LAT = 512
ROPE = 64
VH = 128
ROWS = 128
CAP = 64


def per_device(
    queries,
    cache,
    lengths,
    w_uv,
    w_o,
    x_in,
    norm_gain,
    w_gate,
    w_up,
    w_down,
    expert_ids,
    gate_weights,
    expert_slot,
):
    score_scale = (VH + ROPE) ** (-0.5)
    cache_span = cache.shape[1]
    positions = jnp.arange(cache_span, dtype=jnp.int32)
    valid_mask = positions[None, :] < lengths[:, None]
    scores = (
        jnp.einsum("bhd,btd->bht", queries, cache, preferred_element_type=jnp.float32) * score_scale
    )
    scores = jnp.where(valid_mask[:, None, :], scores, -1e30)
    row_max = jnp.max(scores, axis=2)
    exp_scores = jnp.where(valid_mask[:, None, :], jnp.exp(scores - row_max[:, :, None]), 0.0)
    denominator = jnp.sum(exp_scores, axis=2)
    numerator = jnp.einsum(
        "bht,btc->bhc",
        exp_scores.astype(jnp.bfloat16),
        cache[:, :, :LAT],
        preferred_element_type=jnp.float32,
    )
    latent = (numerator / denominator[:, :, None]).astype(jnp.bfloat16)
    latent = lax.all_gather(latent, "seq", axis=0, tiled=True)
    values = jnp.einsum("bhc,hcj->bhj", latent, w_uv, preferred_element_type=jnp.float32).astype(
        jnp.bfloat16
    )
    attn_term = jnp.einsum("bhj,hjd->bd", values, w_o, preferred_element_type=jnp.float32)
    col_part = lax.psum_scatter(attn_term, "seq", scatter_dimension=1, tiled=True)
    attention = lax.psum(col_part, ("role", "mb"))
    hidden = x_in.astype(jnp.float32) + attention
    squares = lax.psum(jnp.sum(hidden * hidden, axis=1), "seq")
    normed = (hidden * lax.rsqrt(squares[:, None] / D + 1e-06) * norm_gain[None, :]).astype(
        jnp.bfloat16
    )
    seq_count = lax.axis_size("seq")
    pair_count = lax.axis_size("mb")
    pair_index = lax.axis_index("mb")
    expert_count = expert_slot.shape[0]
    expert_range = jnp.arange(expert_count, dtype=jnp.int32)
    named_mask = expert_ids[:, :, None] == expert_range[None, None, :]
    slot_of = jnp.sum(jnp.where(named_mask, expert_slot[None, None, :], 0), axis=2)
    chosen = slot_of[:, :, None] == expert_range[None, None, :]
    member = jnp.any(chosen, axis=1).astype(jnp.int32)
    gate_slot = jnp.sum(jnp.where(chosen, gate_weights[:, :, None], 0.0), axis=1)
    position = jnp.cumsum(member, axis=0) - member
    slot_range = jnp.arange(CAP, dtype=jnp.int32)
    select = (member.T[:, None, :] == 1) & (position.T[:, None, :] == slot_range[None, :, None])
    select_own = lax.dynamic_index_in_dim(
        select.reshape(seq_count, pair_count, CAP, ROWS), pair_index, 1, keepdims=False
    )
    gate_own = lax.dynamic_index_in_dim(
        gate_slot.T.reshape(seq_count, pair_count, ROWS), pair_index, 1, keepdims=False
    )
    select_half = select_own.astype(jnp.bfloat16)
    gathered = lax.all_gather(normed, "seq", axis=1, tiled=True)
    mine = lax.dynamic_index_in_dim(select_half, lax.axis_index("seq"), 0, keepdims=False)
    picked = jnp.dot(mine, gathered, preferred_element_type=jnp.float32).astype(jnp.bfloat16)
    incoming = picked[None]
    item_count = incoming.shape[1]
    rows_in = incoming.reshape(item_count, incoming.shape[2])
    gate_out = jnp.dot(rows_in, w_gate[0], preferred_element_type=jnp.float32)
    up_out = jnp.dot(rows_in, w_up[0], preferred_element_type=jnp.float32)
    activated = (jax.nn.silu(gate_out) * up_out).astype(jnp.bfloat16)
    result = jnp.dot(activated, w_down[0], preferred_element_type=jnp.float32)
    returned = lax.all_to_all(
        result[None].astype(jnp.bfloat16), "seq", split_axis=2, concat_axis=0, tiled=True
    ).astype(jnp.float32)
    mixing = select_own.astype(jnp.float32) * gate_own[:, None, :]
    partial_mix = jnp.einsum("tcb,tcd->bd", mixing, returned, precision=lax.Precision.HIGHEST)
    expert_mix = lax.psum(partial_mix.astype(jnp.bfloat16), ("role", "mb")).astype(jnp.float32)
    return (hidden + expert_mix).astype(jnp.bfloat16)


def solution(mesh):
    in_specs = (
        P(("groups", "seq"), ("role", "mb"), None),
        P(("groups", "seq"), None, None),
        P(("groups", "seq")),
        P(("role", "mb"), None, "seq"),
        P(("role", "mb"), "seq", None),
        P("groups", "seq"),
        P("seq"),
        P(("seq", "mb"), None, "role"),
        P(("seq", "mb"), None, "role"),
        P(("seq", "mb"), "role", None),
        P("groups", None),
        P("groups", None),
        P(),
    )
    out_specs = P("groups", "seq")
    return jax.shard_map(
        per_device, mesh=mesh, in_specs=in_specs, out_specs=out_specs, check_vma=False
    )
```

profile of v0, /device:TPU:0, one launch (start us, length us, event | category | flops | bytes accessed | tf_op | source)
XLA Modules:
  0.0 318.2 jit_solution(6320305931758377276)
XLA Ops:
  6.5 0.0 copy-start
  6.5 0.0 all-gather.2.cloned.1.call-start
  6.5 0.8 iota_compare_fusion.1
  7.4 0.5 copy-done
  7.9 5.5 %fusion.61 = (f32[32,32]{1,0:T(8,128)S(1)}, bf16[32,32,256]{2,1,0:T(8,128)(2,1)S(1)}) fusion(pred[32,256]{1,0:T(8,128)(4,1)S(1)} %iota_compare_fusion.1, bf16[32,32,576]{2,1,0:T(8,128)(2,1)S(1)} %copy-done, bf16[32,256,576]{1,2,0:T(8,128)(2,1)} %param.14), kind=kOutput, calls=%fused_computation.62 | convolution fusion | flops 303563008 | bytes 11153408 | tf_op jit(solution)/shard_map/sub | solution.py:38
  13.3 7.0 %divide_convert_fusion = bf16[32,32,512]{2,1,0:T(8,128)(2,1)} fusion(f32[32,32]{1,0:T(8,128)S(1)} %get-tuple-element.7, bf16[32,256,576]{1,2,0:T(8,128)(2,1)} %param.14, bf16[32,32,256]{2,1,0:T(8,128)(2,1)S(1)} %get-tuple-element.8), kind=kOutput, calls=%fused_computation.15 | convolution fusion | flops 269484032 | bytes 9965568 | tf_op jit(solution)/shard_map/bht,btc->bhc/dot_general | solution.py:40
  20.3 0.0 all-gather.2.cloned.1.call-update
  20.4 0.0 copy-start.4
  20.4 0.0 copy-start.6
  20.4 0.0 copy-start.1
  20.4 0.0 copy-start.3
  20.4 0.0 reduce-scatter.2.cloned.1.call-start
  20.5 83.5 %all-gather.2.cloned.1.call-done = bf16[128,32,512]{2,1,0:T(8,128)(2,1)} async-done(((bf16[32,32,512]{2,1,0:T(8,128)(2,1)}), bf16[128,32,512]{2,1,0:T(8,128)(2,1)}) %all-gather.2.cloned.1.call-update) | async-done | bytes 4194320 | tf_op jit(solution)/shard_map/all_gather | solution.py:47
  104.0 0.0 copy-done.2
  104.0 9.0 %convolution_bitcast_fusion = f32[128,3584]{1,0:T(8,128)} fusion(bf16[32,32,3584]{2,1,0:T(8,128)(2,1)} %param.17, bf16[32,512,32]{1,2,0:T(8,128)(2,1)S(1)} %copy-done.2, bf16[128,32,512]{2,1,0:T(8,128)(2,1)} %all-gather.2.cloned.1.call-done), kind=kOutput, calls=%fused_computation.9 | convolution fusion | flops 1073872896 | bytes 14417920 | tf_op jit(solution)/shard_map/bhj,hjd->bd/dot_general | solution.py:51
  113.0 0.0 reduce-scatter.2.cloned.1.call-update
  113.0 0.0 all-reduce.3.cloned.1.call-start
  113.1 0.0 copy-done.4
  113.1 0.0 copy-done.6
  113.1 0.1 select_reduce_fusion.1
  113.2 0.1 copy.48
  113.3 0.2 reduce_window_sum.11
  113.5 37.7 %reduce-scatter.2.cloned.1.call-done = f32[128,896]{1,0:T(8,128)} async-done(((f32[128,3584]{1,0:T(8,128)}), f32[128,896]{1,0:T(8,128)}) %reduce-scatter.2.cloned.1.call-update) | async-done | bytes 458768 | tf_op jit(solution)/shard_map/reduce_scatter | solution.py:52
  151.2 0.0 all-reduce.3.cloned.1.call-update
  151.3 0.1 copy.49
  151.4 0.1 fusion.47
  151.5 34.2 %all-reduce.3.cloned.1.call-done = f32[128,896]{1,0:T(8,128)} async-done(((f32[128,896]{1,0:T(8,128)}), f32[128,896]{1,0:T(8,128)}) %all-reduce.3.cloned.1.call-update) | async-done | bytes 458768 | tf_op jit(solution)/shard_map/psum | solution.py:53
  185.7 1.2 multiply_reduce_fusion
  186.9 11.8 %psum.22 = f32[128]{0:T(128)S(1)} all-reduce(f32[128]{0:T(128)S(1)} %multiply_reduce_fusion), channel_id=1, replica_groups=mesh['groups'=2,'seq'=4,'role'=2,'mb'=2] {'seq'}, use_global_device_ids=true, to_apply=%region_9.10 | all-reduce | flops 128 | bytes 1024 | tf_op jit(solution)/shard_map/psum | solution.py:55
  198.7 1.1 multiply_convert_fusion
  199.8 18.0 %all_gather.7 = bf16[128,3584]{1,0:T(8,128)(2,1)S(1)} all-gather(bf16[128,896]{1,0:T(8,128)(2,1)S(1)} %multiply_convert_fusion), channel_id=1, replica_groups=mesh['groups'=2,'seq'=4,'role'=2,'mb'=2] {'seq'}, dimensions={1}, use_global_device_ids=true | all-gather | bytes 1146880 | tf_op jit(solution)/shard_map/all_gather | solution.py:79
  217.8 0.3 convolution_convert_fusion
  218.1 4.5 %fusion.7 = f32[64,1024]{1,0:T(8,128)S(1)} fusion(bf16[64,3584]{1,0:T(8,128)(2,1)S(1)} %convolution_convert_fusion, bf16[1,3584,1024]{2,1,0:T(8,128)(2,1)} %param.20), kind=kOutput, calls=%fused_computation.7 | convolution fusion | flops 469762048 | bytes 8060928 | tf_op jit(solution)/shard_map/dot_general | solution.py:85
  222.6 8.6 %fusion.12 = bf16[1,64,3584]{2,1,0:T(8,128)(2,1)} fusion(bf16[1,1024,3584]{2,1,0:T(8,128)(2,1)} %param.22, bf16[64,3584]{1,0:T(8,128)(2,1)S(1)} %convolution_convert_fusion, bf16[1,3584,1024]{2,1,0:T(8,128)(2,1)} %param.21, f32[64,1024]{1,0:T(8,128)S(1)} %fusion.7), kind=kOutput, calls=%fused_computation.12 | convolution fusion | flops 940146688 | bytes 15859712 | tf_op jit(solution)/shard_map/dot_general | solution.py:88
  231.2 4.2 %copy.53 = bf16[1,64,3584]{1,0,2:T(2,128)(2,1)S(1)} copy(bf16[1,64,3584]{2,1,0:T(8,128)(2,1)} %fusion.12) | data formatting | bytes 917504 | tf_op jit(solution)/shard_map/convert_element_type | solution.py:90
  235.4 0.5 broadcast.36
  236.0 20.6 %reduce = bf16[3584,64]{1,0:T(8,128)(2,1)} reduce(bf16[3584,1,64]{2,1,0:T(2,128)(2,1)S(1)} %bitcast.64, bf16[]{:T(256)} %broadcast.36), dimensions={1}, to_apply=%bitcast.54.reduce_sub_computation | reduce | bytes 917506
  256.6 2.8 reshape.46
  259.4 4.1 %all-to-all-start = ((bf16[4,2,28672]{2,1,0:T(2,128)(2,1)}), bf16[4,2,28672]{2,1,0:T(2,128)(2,1)}, u32[]{:S(2)}, u32[]{:S(2)}) async-start(bf16[4,2,28672]{2,1,0:T(2,128)(2,1)} %reshape.46), calls=%async_computation.1 | async-start | bytes 917504 | tf_op jit(solution)/shard_map/all_to_all | solution.py:89
  263.6 0.0 all-reduce.5.cloned.1.call-start
  263.6 9.6 %all-to-all-done = bf16[4,2,28672]{2,1,0:T(2,128)(2,1)} async-done(((bf16[4,2,28672]{2,1,0:T(2,128)(2,1)}), bf16[4,2,28672]{2,1,0:T(2,128)(2,1)}, u32[]{:S(2)}, u32[]{:S(2)}) %all-to-all-start) | async-done | bytes 458784 | tf_op jit(solution)/shard_map/all_to_all | solution.py:89
  273.2 2.4 reshape.47
  275.6 1.0 copy.58
  276.7 1.5 copy.55
  278.2 1.1 fusion.24
  279.3 0.0 all-reduce.5.cloned.1.call-update
  279.3 30.5 %all-reduce.5.cloned.1.call-done = bf16[128,896]{1,0:T(8,128)(2,1)} async-done(((bf16[128,896]{1,0:T(8,128)(2,1)}), bf16[128,896]{1,0:T(8,128)(2,1)}) %all-reduce.5.cloned.1.call-update) | async-done | bytes 229392 | tf_op jit(solution)/shard_map/psum | solution.py:94
  309.8 1.9 add_convert_fusion
  (15 shorter events, 0.2 us)
Async XLA Ops:
  6.5 1.3 copy-start
  6.5 97.4 %all-gather.2.cloned.1.call-start = ((), (), s32[]{:S(2)}) async-start(), calls=%async_computation.2 | async-start | bytes 5242880 | tf_op jit(solution)/shard_map/all_gather | solution.py:47
  13.3 90.6 %copy-start.2 = (bf16[32,512,32]{1,2,0:T(8,128)(2,1)S(1)}, bf16[32,512,32]{1,2,0:T(8,128)(2,1)}, u32[]{:S(2)}) copy-start(bf16[32,512,32]{1,2,0:T(8,128)(2,1)} %param.16) | copy-start | bytes 3145732
  20.4 92.7 %copy-start.4 = (s32[128,2]{0,1:T(2,128)S(1)}, s32[128,2]{0,1:T(2,128)}, u32[]{:S(2)}) copy-start(s32[128,2]{0,1:T(2,128)} %param.23) | copy-start | bytes 3076
  20.4 92.7 %copy-start.6 = (s32[8]{0:T(128)S(1)}, s32[8]{0:T(128)}, u32[]{:S(2)}) copy-start(s32[8]{0:T(128)} %param.25) | copy-start | bytes 100
  20.4 165.3 %copy-start.1 = (bf16[128,896]{1,0:T(8,128)(2,1)S(1)}, bf16[128,896]{1,0:T(8,128)(2,1)}, u32[]{:S(2)}) copy-start(bf16[128,896]{1,0:T(8,128)(2,1)} %param.18) | copy-start | bytes 688132
  20.4 178.3 %copy-start.3 = (f32[896]{0:T(1024)S(1)}, f32[896]{0:T(1024)}, u32[]{:S(2)}) copy-start(f32[896]{0:T(1024)} %param.19) | copy-start | bytes 10756
  20.4 130.8 %reduce-scatter.2.cloned.1.call-start = ((), (), s32[]{:S(2)}) async-start(), calls=%async_computation.3 | async-start | bytes 2293760 | tf_op jit(solution)/shard_map/reduce_scatter | solution.py:52
  113.0 72.7 %all-reduce.3.cloned.1.call-start = ((), (), s32[]{:S(2)}) async-start(), calls=%async_computation.4 | async-start | bytes 917504 | tf_op jit(solution)/shard_map/psum | solution.py:53
  231.2 32.4 %copy-start.5 = (f32[128,2]{0,1:T(2,128)S(1)}, f32[128,2]{0,1:T(2,128)}, u32[]{:S(2)}) copy-start(f32[128,2]{0,1:T(2,128)} %param.24) | copy-start | bytes 3076
  259.4 13.8 %all-to-all-start = ((bf16[4,2,28672]{2,1,0:T(2,128)(2,1)}), bf16[4,2,28672]{2,1,0:T(2,128)(2,1)}, u32[]{:S(2)}, u32[]{:S(2)}) async-start(bf16[4,2,28672]{2,1,0:T(2,128)(2,1)} %reshape.46), calls=%async_computation.1 | async-start | bytes 917504 | tf_op jit(solution)/shard_map/all_to_all | solution.py:89
  263.6 46.3 %all-reduce.5.cloned.1.call-start = ((), (), s32[]{:S(2)}) async-start(), calls=%async_computation.5 | async-start | bytes 458752 | tf_op jit(solution)/shard_map/psum | solution.py:94
Sparse Core Ops, SparseCore 0:
  20.5 83.4 all-gather.1
  113.1 37.9 reduce-scatter.1
  153.5 32.1 all-reduce.2
  279.5 30.3 all-reduce.4
where the time goes:
time: 319 us; the launch traced here: 318 us
  waiting for transfers between devices  196 us (61%)
  matrix products  36 us (11%)
  blocking collectives  29.8 us (9%)
  other arithmetic  26 us (8%)
  local copies, waits for them, and re-layouts  13.4 us (4%)
  between operations  13.3 us (4%)
  starting transfers between devices  4.25 us (1%)
    all_gather x1, waiting for transfers between devices, per_device(): latent = lax.all_gather(latent, 'seq', axis=0, tiled=True)  83.5 us
    reduce_scatter x1, waiting for transfers between devices, per_device(): lax.psum_scatter(attn_term, 'seq', scatter_dimension=1, tiled=True)  37.7 us
    psum x1, waiting for transfers between devices, per_device(): attention = lax.psum(col_part, ('role', 'mb'))  34.2 us
    psum x1, waiting for transfers between devices, per_device(): lax.psum(partial_mix.astype(jnp.bfloat16), ('role', 'mb'))  30.5 us
    unnamed x1, other arithmetic  20.6 us
    all_gather x1, blocking collectives, per_device(): gathered = lax.all_gather(normed, 'seq', axis=1, tiled=True)  18 us
    psum x1, blocking collectives, per_device(): squares = lax.psum(jnp.sum(hidden * hidden, axis=1), 'seq')  11.8 us
    all_to_all x1, waiting for transfers between devices, per_device(): lax.all_to_all(result[None].astype(jnp.bfloat16), 'seq', split_axis=2, co...  9.55 us
  transfers between devices with their start and end apart: 5, of which 5 were waited for; matrix products, arithmetic and copies ran while one was open for 0% of the time, Pallas kernels for 0%

commit v1 on v0

--- a/solution.py
+++ b/solution.py
@@ -9,6 +9,17 @@
 VH = 128
 ROWS = 128
 CAP = 64
+
+
+def gather_around(x, axis, dim):
+    ways = lax.axis_size(axis)
+    pieces = [x]
+    for far in range(1, ways):
+        pieces.append(
+            lax.ppermute(pieces[far - 1], axis, [(d, (d - 1) % ways) for d in range(ways)])
+        )
+    line = jnp.concatenate(pieces, axis=dim)
+    return jnp.roll(line, lax.axis_index(axis) * x.shape[dim], axis=dim)
 
 
 def per_device(
@@ -76,7 +87,7 @@
         gate_slot.T.reshape(seq_count, pair_count, ROWS), pair_index, 1, keepdims=False
     )
     select_half = select_own.astype(jnp.bfloat16)
-    gathered = lax.all_gather(normed, "seq", axis=1, tiled=True)
+    gathered = gather_around(normed, "seq", 1)
     mine = lax.dynamic_index_in_dim(select_half, lax.axis_index("seq"), 0, keepdims=False)
     picked = jnp.dot(mine, gathered, preferred_element_type=jnp.float32).astype(jnp.bfloat16)
     incoming = picked[None]

time: 319 us -> 328 us (1.028)
  waiting for transfers between devices: 196 us -> 215 us
  blocking collectives: 29.8 us -> 11.8 us
  local copies, waits for them, and re-layouts: 13.4 us -> 18.5 us
    ppermute x0 -> x3, waiting for transfers between devices: none -> 18.6 us  [gather_around(): lax.ppermute(pieces[far - 1], axis, [(d, (d - 1) % ways) for d in range(w...]
    all_gather x1 -> x0, blocking collectives: 18 us -> none  [per_device(): gathered = lax.all_gather(normed, 'seq', axis=1, tiled=True)]
    unnamed x18 -> x26, local copies, waits for them, and re-layouts: 7.37 us -> 11.8 us
    unnamed x1 -> x2, other arithmetic: 20.6 us -> 22.5 us
  transfers between devices with their start and end apart: 5 -> 8, of which waited for: 5 -> 8; matrix products, arithmetic and copies ran while one was open for 0% -> 1% of each run, Pallas kernels for 0% -> 0%
where the time goes in v1:
time: 328 us
  waiting for transfers between devices  215 us (66%)
  matrix products  37.3 us (11%)
  other arithmetic  26.5 us (8%)
  local copies, waits for them, and re-layouts  18.5 us (6%)
  between operations  13.3 us (4%)
  blocking collectives  11.8 us (4%)
  starting transfers between devices  5.51 us (2%)
    all_gather x1, waiting for transfers between devices, per_device(): latent = lax.all_gather(latent, 'seq', axis=0, tiled=True)  83.6 us
    reduce_scatter x1, waiting for transfers between devices, per_device(): lax.psum_scatter(attn_term, 'seq', scatter_dimension=1, tiled=True)  38.1 us
    psum x1, waiting for transfers between devices, per_device(): attention = lax.psum(col_part, ('role', 'mb'))  34.4 us
    psum x1, waiting for transfers between devices, per_device(): lax.psum(partial_mix.astype(jnp.bfloat16), ('role', 'mb'))  30.4 us
    unnamed x2, other arithmetic  22.5 us
    ppermute x3, waiting for transfers between devices, gather_around(): lax.ppermute(pieces[far - 1], axis, [(d, (d - 1) % ways) for d in range(w...  18.6 us
    psum x1, blocking collectives, per_device(): squares = lax.psum(jnp.sum(hidden * hidden, axis=1), 'seq')  11.8 us
    unnamed x26, local copies, waits for them, and re-layouts  11.8 us
  transfers between devices with their start and end apart: 8, of which 8 were waited for; matrix products, arithmetic and copies ran while one was open for 1% of the time, Pallas kernels for 0%

profile of v1, /device:TPU:0, one launch (start us, length us, event | category | flops | bytes accessed | tf_op | source)
XLA Modules:
  0.0 327.8 jit_solution(1261630682481605524)
XLA Ops:
  6.5 0.8 iota_compare_fusion.1
  7.4 0.5 copy-done
  7.9 5.5 %fusion.62 = (f32[32,32]{1,0:T(8,128)S(1)}, bf16[32,32,256]{2,1,0:T(8,128)(2,1)S(1)}) fusion(pred[32,256]{1,0:T(8,128)(4,1)S(1)} %iota_compare_fusion.1, bf16[32,32,576]{2,1,0:T(8,128)(2,1)S(1)} %copy-done, bf16[32,256,576]{1,2,0:T(8,128)(2,1)} %param.14), kind=kOutput, calls=%fused_computation.71 | convolution fusion | flops 303563008 | bytes 11153408 | tf_op jit(solution)/shard_map/sub | solution.py:49
  13.3 7.0 %divide_convert_fusion = bf16[32,32,512]{2,1,0:T(8,128)(2,1)} fusion(f32[32,32]{1,0:T(8,128)S(1)} %get-tuple-element.9, bf16[32,256,576]{1,2,0:T(8,128)(2,1)} %param.14, bf16[32,32,256]{2,1,0:T(8,128)(2,1)S(1)} %get-tuple-element.10), kind=kOutput, calls=%fused_computation.15 | convolution fusion | flops 269484032 | bytes 9965568 | tf_op jit(solution)/shard_map/bht,btc->bhc/dot_general | solution.py:51
  20.3 0.0 all-gather.2.cloned.1.call-update
  20.4 0.0 reduce-scatter.2.cloned.1.call-start
  20.4 83.6 %all-gather.2.cloned.1.call-done = bf16[128,32,512]{2,1,0:T(8,128)(2,1)} async-done(((bf16[32,32,512]{2,1,0:T(8,128)(2,1)}), bf16[128,32,512]{2,1,0:T(8,128)(2,1)}) %all-gather.2.cloned.1.call-update) | async-done | bytes 4194320 | tf_op jit(solution)/shard_map/all_gather | solution.py:58
  104.0 9.0 %convolution_bitcast_fusion = f32[128,3584]{1,0:T(8,128)} fusion(bf16[32,32,3584]{2,1,0:T(8,128)(2,1)} %param.17, bf16[32,512,32]{1,2,0:T(8,128)(2,1)S(1)} %copy-done.3, bf16[128,32,512]{2,1,0:T(8,128)(2,1)} %all-gather.2.cloned.1.call-done), kind=kOutput, calls=%fused_computation.9 | convolution fusion | flops 1073872896 | bytes 14417920 | tf_op jit(solution)/shard_map/bhj,hjd->bd/dot_general | solution.py:62
  113.0 0.0 reduce-scatter.2.cloned.1.call-update
  113.0 0.0 all-reduce.3.cloned.1.call-start
  113.1 38.1 %reduce-scatter.2.cloned.1.call-done = f32[128,896]{1,0:T(8,128)} async-done(((f32[128,3584]{1,0:T(8,128)}), f32[128,896]{1,0:T(8,128)}) %reduce-scatter.2.cloned.1.call-update) | async-done | bytes 458768 | tf_op jit(solution)/shard_map/reduce_scatter | solution.py:63
  151.2 0.0 all-reduce.3.cloned.1.call-update
  151.2 0.1 select_reduce_fusion.1
  151.3 34.4 %all-reduce.3.cloned.1.call-done = f32[128,896]{1,0:T(8,128)} async-done(((f32[128,896]{1,0:T(8,128)}), f32[128,896]{1,0:T(8,128)}) %all-reduce.3.cloned.1.call-update) | async-done | bytes 458768 | tf_op jit(solution)/shard_map/psum | solution.py:64
  185.7 1.2 multiply_reduce_fusion
  186.9 11.8 %psum.22 = f32[128]{0:T(128)S(1)} all-reduce(f32[128]{0:T(128)S(1)} %multiply_reduce_fusion), channel_id=1, replica_groups=mesh['groups'=2,'seq'=4,'role'=2,'mb'=2] {'seq'}, use_global_device_ids=true, to_apply=%region_9.10 | all-reduce | flops 128 | bytes 1024 | tf_op jit(solution)/shard_map/psum | solution.py:66
  198.7 1.8 constant_dynamic-update-slice_fusion.7
  200.5 0.1 copy.48
  200.7 0.2 reduce_window_sum.11
  200.9 7.6 %collective-permute-done = bf16[128,896]{1,0:T(8,128)(2,1)S(1)} collective-permute-done((bf16[128,896]{1,0:T(8,128)(2,1)S(1)}, bf16[128,896]{1,0:T(8,128)(2,1)S(1)}, u32[]{:S(2)}, u32[]{:S(2)}) %collective-permute-start) | collective-permute-done | bytes 229408 | tf_op jit(solution)/shard_map/ppermute | solution.py:19
  208.6 0.1 copy.49
  208.7 0.1 fusion.48
  208.8 7.5 %collective-permute-done.1 = bf16[128,896]{1,0:T(8,128)(2,1)S(1)} collective-permute-done((bf16[128,896]{1,0:T(8,128)(2,1)S(1)}, bf16[128,896]{1,0:T(8,128)(2,1)S(1)}, u32[]{:S(2)}, u32[]{:S(2)}) %collective-permute-start.1) | collective-permute-done | bytes 229408 | tf_op jit(solution)/shard_map/ppermute | solution.py:19
  216.3 1.2 collective-permute-start.2
  217.5 0.7 constant_dynamic-update-slice_fusion.6
  218.2 0.7 constant_dynamic-update-slice_fusion.5
  219.0 3.4 %collective-permute-done.2 = bf16[128,896]{1,0:T(8,128)(2,1)S(1)} collective-permute-done((bf16[128,896]{1,0:T(8,128)(2,1)S(1)}, bf16[128,896]{1,0:T(8,128)(2,1)S(1)}, u32[]{:S(2)}, u32[]{:S(2)}) %collective-permute-start.2) | collective-permute-done | bytes 229408 | tf_op jit(solution)/shard_map/ppermute | solution.py:19
  222.4 0.7 constant_dynamic-update-slice_fusion.4
  223.1 0.7 constant_dynamic-update-slice_fusion.3
  223.8 0.7 constant_dynamic-update-slice_fusion.2
  224.5 0.8 constant_dynamic-update-slice_fusion.1
  225.3 0.7 constant_dynamic-update-slice_fusion
  226.0 1.6 convolution_convert_fusion
  227.7 4.5 %fusion.7 = f32[64,1024]{1,0:T(8,128)S(1)} fusion(bf16[64,3584]{1,0:T(8,128)(2,1)S(1)} %convolution_convert_fusion, bf16[1,3584,1024]{2,1,0:T(8,128)(2,1)} %param.20), kind=kOutput, calls=%fused_computation.7 | convolution fusion | flops 469762048 | bytes 8060928 | tf_op jit(solution)/shard_map/dot_general | solution.py:96
  232.1 8.6 %fusion.12 = bf16[1,64,3584]{2,1,0:T(8,128)(2,1)} fusion(bf16[1,1024,3584]{2,1,0:T(8,128)(2,1)} %param.22, bf16[64,3584]{1,0:T(8,128)(2,1)S(1)} %convolution_convert_fusion, bf16[1,3584,1024]{2,1,0:T(8,128)(2,1)} %param.21, f32[64,1024]{1,0:T(8,128)S(1)} %fusion.7), kind=kOutput, calls=%fused_computation.12 | convolution fusion | flops 940146688 | bytes 15859712 | tf_op jit(solution)/shard_map/dot_general | solution.py:99
  240.8 4.2 %copy.53 = bf16[1,64,3584]{1,0,2:T(2,128)(2,1)S(1)} copy(bf16[1,64,3584]{2,1,0:T(8,128)(2,1)} %fusion.12) | data formatting | bytes 917504 | tf_op jit(solution)/shard_map/convert_element_type | solution.py:101
  245.0 0.5 broadcast.36
  245.5 20.6 %reduce = bf16[3584,64]{1,0:T(8,128)(2,1)} reduce(bf16[3584,1,64]{2,1,0:T(2,128)(2,1)S(1)} %bitcast.63, bf16[]{:T(256)} %broadcast.36), dimensions={1}, to_apply=%bitcast.54.reduce_sub_computation | reduce | bytes 917506
  266.1 2.8 reshape.46
  268.9 4.2 %all-to-all-start = ((bf16[4,2,28672]{2,1,0:T(2,128)(2,1)}), bf16[4,2,28672]{2,1,0:T(2,128)(2,1)}, u32[]{:S(2)}, u32[]{:S(2)}) async-start(bf16[4,2,28672]{2,1,0:T(2,128)(2,1)} %reshape.46), calls=%async_computation.1 | async-start | bytes 917504 | tf_op jit(solution)/shard_map/all_to_all | solution.py:100
  273.2 9.7 %all-to-all-done = bf16[4,2,28672]{2,1,0:T(2,128)(2,1)} async-done(((bf16[4,2,28672]{2,1,0:T(2,128)(2,1)}), bf16[4,2,28672]{2,1,0:T(2,128)(2,1)}, u32[]{:S(2)}, u32[]{:S(2)}) %all-to-all-start) | async-done | bytes 458784 | tf_op jit(solution)/shard_map/all_to_all | solution.py:100
  282.9 2.4 reshape.47
  285.3 1.0 copy.58
  286.4 1.6 copy.55
  287.9 1.1 fusion.24
  289.1 0.0 all-reduce.5.cloned.1.call-update
  289.1 30.4 %all-reduce.5.cloned.1.call-done = bf16[128,896]{1,0:T(8,128)(2,1)} async-done(((bf16[128,896]{1,0:T(8,128)(2,1)}), bf16[128,896]{1,0:T(8,128)(2,1)}) %all-reduce.5.cloned.1.call-update) | async-done | bytes 229392 | tf_op jit(solution)/shard_map/psum | solution.py:105
  319.5 1.7 add_convert_fusion
  (29 shorter events, 0.2 us)
Async XLA Ops:
  6.5 1.3 copy-start
  6.5 97.4 %all-gather.2.cloned.1.call-start = ((), (), s32[]{:S(2)}) async-start(), calls=%async_computation.2 | async-start | bytes 5242880 | tf_op jit(solution)/shard_map/all_gather | solution.py:58
  13.3 90.6 %copy-start.3 = (bf16[32,512,32]{1,2,0:T(8,128)(2,1)S(1)}, bf16[32,512,32]{1,2,0:T(8,128)(2,1)}, u32[]{:S(2)}) copy-start(bf16[32,512,32]{1,2,0:T(8,128)(2,1)} %param.16) | copy-start | bytes 3145732
  20.4 130.8 %reduce-scatter.2.cloned.1.call-start = ((), (), s32[]{:S(2)}) async-start(), calls=%async_computation.3 | async-start | bytes 2293760 | tf_op jit(solution)/shard_map/reduce_scatter | solution.py:63
  113.0 38.2 %copy-start.5 = (s32[128,2]{0,1:T(2,128)S(1)}, s32[128,2]{0,1:T(2,128)}, u32[]{:S(2)}) copy-start(s32[128,2]{0,1:T(2,128)} %param.23) | copy-start | bytes 3076
  113.0 38.2 %copy-start.7 = (s32[8]{0:T(128)S(1)}, s32[8]{0:T(128)}, u32[]{:S(2)}) copy-start(s32[8]{0:T(128)} %param.25) | copy-start | bytes 100
  113.0 72.7 %copy-start.2 = (bf16[128,896]{1,0:T(8,128)(2,1)S(1)}, bf16[128,896]{1,0:T(8,128)(2,1)}, u32[]{:S(2)}) copy-start(bf16[128,896]{1,0:T(8,128)(2,1)} %param.18) | copy-start | bytes 688132
  113.0 85.7 %copy-start.4 = (f32[896]{0:T(1024)S(1)}, f32[896]{0:T(1024)}, u32[]{:S(2)}) copy-start(f32[896]{0:T(1024)} %param.19) | copy-start | bytes 10756
  113.0 72.7 %all-reduce.3.cloned.1.call-start = ((), (), s32[]{:S(2)}) async-start(), calls=%async_computation.4 | async-start | bytes 917504 | tf_op jit(solution)/shard_map/psum | solution.py:64
  200.5 8.0 %collective-permute-start = (bf16[128,896]{1,0:T(8,128)(2,1)S(1)}, bf16[128,896]{1,0:T(8,128)(2,1)S(1)}, u32[]{:S(2)}, u32[]{:S(2)}) collective-permute-start(bf16[128,896]{1,0:T(8,128)(2,1)S(1)} %get-tuple-element.6), channel_id=1, source_target_pairs={{0,12},{4,0},{8,4},{12,8},{1,13},{5,1},{9,5},{13,9},{2,14},{6,2},{... | collective-permute-start | bytes 688136 | tf_op jit(solution)/shard_map/ppermute | solution.py:19
  208.5 7.8 %collective-permute-start.1 = (bf16[128,896]{1,0:T(8,128)(2,1)S(1)}, bf16[128,896]{1,0:T(8,128)(2,1)S(1)}, u32[]{:S(2)}, u32[]{:S(2)}) collective-permute-start(bf16[128,896]{1,0:T(8,128)(2,1)S(1)} %collective-permute-done), channel_id=1, source_target_pairs={{0,12},{4,0},{8,4},{12,8},{1,13},{5,1},{9,5},{13,9},{2,14},{6,2},{... | collective-permute-start | bytes 688136 | tf_op jit(solution)/shard_map/ppermute | solution.py:19
  216.3 6.0 %collective-permute-start.2 = (bf16[128,896]{1,0:T(8,128)(2,1)S(1)}, bf16[128,896]{1,0:T(8,128)(2,1)S(1)}, u32[]{:S(2)}, u32[]{:S(2)}) collective-permute-start(bf16[128,896]{1,0:T(8,128)(2,1)S(1)} %collective-permute-done.1), channel_id=1, source_target_pairs={{0,12},{4,0},{8,4},{12,8},{1,13},{5,1},{9,5},{13,9},{2,14},{6,2},{... | collective-permute-start | bytes 688136 | tf_op jit(solution)/shard_map/ppermute | solution.py:19
  245.5 27.7 %copy-start.6 = (f32[128,2]{0,1:T(2,128)S(1)}, f32[128,2]{0,1:T(2,128)}, u32[]{:S(2)}) copy-start(f32[128,2]{0,1:T(2,128)} %param.24) | copy-start | bytes 3076
  268.9 13.9 %all-to-all-start = ((bf16[4,2,28672]{2,1,0:T(2,128)(2,1)}), bf16[4,2,28672]{2,1,0:T(2,128)(2,1)}, u32[]{:S(2)}, u32[]{:S(2)}) async-start(bf16[4,2,28672]{2,1,0:T(2,128)(2,1)} %reshape.46), calls=%async_computation.1 | async-start | bytes 917504 | tf_op jit(solution)/shard_map/all_to_all | solution.py:100
  273.2 46.3 %all-reduce.5.cloned.1.call-start = ((), (), s32[]{:S(2)}) async-start(), calls=%async_computation.5 | async-start | bytes 458752 | tf_op jit(solution)/shard_map/psum | solution.py:105
  286.4 33.2 %copy-start.1 = (f32[128,896]{1,0:T(8,128)S(1)}, f32[128,896]{1,0:T(8,128)}, u32[]{:S(2)}) copy-start(f32[128,896]{1,0:T(8,128)} %all-reduce.3.cloned.1.call-done) | copy-start | bytes 1376260
Sparse Core Ops, SparseCore 0:
  20.5 83.4 all-gather.1
  113.2 37.9 reduce-scatter.1
  153.6 32.1 all-reduce.2
  289.2 30.2 all-reduce.4
